TPU v7x, 128 devices: a whole 4x4x4 slice. The times are simulated.
128 devices in a mesh: gx: 2 (over core), gy: 64 (over z, y, x).
Axes of the slice: x: 4, y: 4, z: 4, core: 2. Of those that a mesh axis runs over, the one named last changes fastest.
Arguments:
- right_side: float32 [128, 16384], P('gx', 'gy'), may hold values from -34 to 34, as said below
- initial: float32 [128, 16384], P('gx', 'gy'), may hold values from -0.6 to 0.6
- reaction: float32 [128, 16384], P('gx', 'gy'), may hold values from 0.05 to 0.5
- velocity_x: float32 [128, 16384], P('gx', 'gy'), may hold values from -1 to 1
- velocity_y: float32 [128, 16384], P('gx', 'gy'), may hold values from -1 to 1
Outputs:
- solution: float32 [128, 16384], P('gx', 'gy')
- residual: float32 [128, 16384], P('gx', 'gy')
Inputs may be any that keep to these rules, and one draw needn't show every extreme that they name: right_side is noise bounded by 4 in size times an envelope 0.5 + 8 g, where g is a periodic Gaussian bump of one device block's width along each dimension centred at a drawn position, so its entries lie within -34 and 34.
All inputs are finite; a program needn't handle non-finite values.
Results may differ from a plain program's by a relative error of at most 0.0075.
Values sent between devices are 32-bit elements.
A program may use at most 64 MiB of HBM per device.

v0:
```python
import jax
import jax.numpy as jnp
from jax import lax
from jax.sharding import Mesh
from jax.sharding import PartitionSpec as P

RESTART = 15
GX_GY = ("gx", "gy_0", "gy_1", "gy_2")
GY = ("gy_0", "gy_1", "gy_2")


def padded_2(cells, sides, width, closed):
    for axis, dim in sides:
        count = lax.axis_size(axis)
        ends = count if closed else count - 1
        head = lax.slice_in_dim(cells, 0, width, axis=dim)
        tail = lax.slice_in_dim(cells, cells.shape[dim] - width, cells.shape[dim], axis=dim)
        cells = jnp.concatenate(
            [
                lax.ppermute(tail, axis, [(i, (i + 1) % count) for i in range(ends)]),
                cells,
                lax.ppermute(head, axis, [((i + 1) % count, i) for i in range(ends)]),
            ],
            axis=dim,
        )
    return cells


def one_axis_at_a_time(x, axes):
    for axis in axes:
        x = lax.psum(x, axis)
    return x


def shifted(padded, offset, dimension, extent):
    row_start = 2 + offset if dimension == 0 else 2
    column_start = 2 + offset if dimension == 1 else 2
    return lax.slice(
        padded, (row_start, column_start), (row_start + extent[0], column_start + extent[1])
    )


def first_diff(padded, dimension, extent):
    outer = shifted(padded, -2, dimension, extent) - shifted(padded, 2, dimension, extent)
    inner = shifted(padded, 1, dimension, extent) - shifted(padded, -1, dimension, extent)
    return (outer + 8.0 * inner) / 12.0


def second_diff(padded, dimension, extent):
    inner = shifted(padded, 1, dimension, extent) + shifted(padded, -1, dimension, extent)
    outer = shifted(padded, 2, dimension, extent) + shifted(padded, -2, dimension, extent)
    return (16.0 * inner - outer - 30.0 * shifted(padded, 0, dimension, extent)) / 12.0


def apply_operator(field, padded_field, padded_speeds, reaction, velocity_x, velocity_y):
    extent = field.shape
    diffusion = second_diff(padded_field, 0, extent) + second_diff(padded_field, 1, extent)
    advect_x = 0.5 * (
        velocity_x * first_diff(padded_field, 0, extent)
        + first_diff(padded_speeds[0] * padded_field, 0, extent)
    )
    advect_y = 0.5 * (
        velocity_y * first_diff(padded_field, 1, extent)
        + first_diff(padded_speeds[1] * padded_field, 1, extent)
    )
    return reaction * field - diffusion + advect_x + advect_y


def least_squares(hessenberg, beta):
    columns_total = hessenberg.shape[1]
    target = jnp.where(jnp.arange(columns_total + 1) == 0, beta, 0.0)

    def rotate(column, carried):
        upper, target = carried
        top_row = upper[column]
        next_row = upper[column + 1]
        diagonal_entry = top_row[column]
        below_entry = next_row[column]
        radius = jnp.sqrt(diagonal_entry * diagonal_entry + below_entry * below_entry)
        cosine = diagonal_entry / radius
        sine_value = below_entry / radius
        upper = upper.at[column].set(cosine * top_row + sine_value * next_row)
        upper = upper.at[column + 1].set(cosine * next_row - sine_value * top_row)
        upper_value = target[column]
        lower_value = target[column + 1]
        target = target.at[column].set(cosine * upper_value + sine_value * lower_value)
        target = target.at[column + 1].set(cosine * lower_value - sine_value * upper_value)
        return (upper, target)

    upper, target = lax.fori_loop(0, columns_total, rotate, (hessenberg, target))

    def substitute(count, weights):
        row_index = columns_total - 1 - count
        known = jnp.sum(upper[row_index] * weights)
        return weights.at[row_index].set((target[row_index] - known) / upper[row_index, row_index])

    return lax.fori_loop(0, columns_total, substitute, jnp.zeros((columns_total,), jnp.float32))


def per_device(right_side, initial, reaction, velocity_x, velocity_y):
    row_count, column_count = right_side.shape
    speeds = jnp.stack([velocity_x, velocity_y])
    padded_speeds = padded_2(speeds, (("gx", 1), (GY, 2)), 2, True)

    def operator_on(field):
        padded_field = padded_2(field, (("gx", 0), (GY, 1)), 2, True)
        return apply_operator(field, padded_field, padded_speeds, reaction, velocity_x, velocity_y)

    start_residual = right_side - operator_on(initial)
    start_square = one_axis_at_a_time(jnp.sum(start_residual * start_residual), GX_GY)
    beta = jnp.sqrt(start_square)
    basis = jnp.zeros((RESTART + 1, row_count, column_count), jnp.float32)
    basis = basis.at[0].set(start_residual / beta)
    hessenberg = jnp.zeros((RESTART + 1, RESTART), jnp.float32)
    positions = jnp.arange(RESTART + 1)

    def arnoldi(column, carried):
        basis, hessenberg = carried
        current = lax.dynamic_index_in_dim(basis, column, 0, keepdims=False)
        applied = operator_on(current)
        local_projection = jnp.einsum("kxy,xy->k", basis, applied, precision=lax.Precision.HIGHEST)
        projection, applied_square = (
            one_axis_at_a_time(local_projection, GX_GY),
            one_axis_at_a_time(jnp.sum(applied * applied), GX_GY),
        )
        applied = applied - jnp.einsum(
            "k,kxy->xy", projection, basis, precision=lax.Precision.HIGHEST
        )
        length = jnp.sqrt(applied_square - jnp.sum(projection * projection))
        entries = jnp.where(positions == column + 1, length, projection)
        hessenberg = lax.dynamic_update_slice(hessenberg, entries[:, None], (0, column))
        basis = lax.dynamic_update_index_in_dim(basis, applied / length, column + 1, 0)
        return (basis, hessenberg)

    basis, hessenberg = lax.fori_loop(0, RESTART, arnoldi, (basis, hessenberg))
    weights = least_squares(hessenberg, beta)
    padded_weights = jnp.concatenate([weights, jnp.zeros((1,), jnp.float32)])
    solution = initial + jnp.einsum(
        "k,kxy->xy", padded_weights, basis, precision=lax.Precision.HIGHEST
    )
    leftover = jnp.where(positions == 0, beta, 0.0) - jnp.dot(
        hessenberg, weights, precision=lax.Precision.HIGHEST
    )
    residual = jnp.einsum("k,kxy->xy", leftover, basis, precision=lax.Precision.HIGHEST)
    return (solution, residual)


def solution(mesh):
    torus = Mesh(mesh.devices.reshape(mesh.shape["gx"], 4, 4, 4), ("gx", "gy_0", "gy_1", "gy_2"))
    placed = (P("gx", GY), P("gx", GY), P("gx", GY), P("gx", GY), P("gx", GY))
    return jax.shard_map(
        per_device,
        mesh=torus,
        in_specs=placed,
        out_specs=(P("gx", GY), P("gx", GY)),
        check_vma=False,
    )
```

profile of v0, /device:TPU:0, one launch (start us, length us, event | category | flops | bytes accessed | tf_op | source)
XLA Modules:
  0.0 1035.0 jit_solution(6680681950074222786)
XLA Ops:
  3.4 8.8 collective-permute-start.6
  44.3 16.7 %psum.143 = f32[]{:T(128)} all-reduce(f32[]{:T(128)} %psum.142), channel_id=1, replica_groups=mesh['gx'=2,'gy_0'=4,'gy_1'=4,'gy_2'=4] {'gy_2'}, use_global_device_ids=true, to_apply=%region_4.0 | all-reduce | flops 1 | bytes 8 | tf_op jit(solution)/shard_map/psum | solution.py:31
  61.8 747.0 %while.56 = (s32[]{:T(128)}, f32[16,64,256]{2,1,0:T(8,128)S(1)}, f32[16,15]{0,1:T(8,128)S(1)}, f32[64,256]{1,0:T(8,128)S(1)}, f32[64,256]{1,0:T(8,128)S(1)}, /*i...) while((s32[]{:T(128)}, f32[16,64,256]{2,1,0:T(8,128)S(1)}, ...), condition=%wide.region_16.0_spmd.clone, body=%wide.region_5.16_spmd.clone.sunk | while | flops 7373337 | bytes 4410527 | solution.py:135
  78.8 8.3 all-reduce.10
  87.2 8.3 all-reduce.11
  95.5 9.4 all-reduce.12
  128.9 8.3 all-reduce.10
  137.2 8.3 all-reduce.11
  145.6 9.4 all-reduce.12
  178.9 8.3 all-reduce.10
  187.3 8.3 all-reduce.11
  195.6 9.4 all-reduce.12
  229.0 8.3 all-reduce.10
  237.3 8.3 all-reduce.11
  245.7 9.4 all-reduce.12
  279.0 8.3 all-reduce.10
  287.4 8.3 all-reduce.11
  295.7 9.4 all-reduce.12
  329.1 8.3 all-reduce.10
  337.4 8.3 all-reduce.11
  345.8 9.4 all-reduce.12
  379.1 8.3 all-reduce.10
  387.5 8.3 all-reduce.11
  395.8 9.4 all-reduce.12
  429.2 8.3 all-reduce.10
  437.5 8.3 all-reduce.11
  445.9 9.4 all-reduce.12
  479.2 8.3 all-reduce.10
  487.6 8.3 all-reduce.11
  495.9 9.4 all-reduce.12
  529.3 8.3 all-reduce.10
  537.6 8.3 all-reduce.11
  546.0 9.4 all-reduce.12
  579.3 8.3 all-reduce.10
  587.7 8.3 all-reduce.11
  596.0 9.4 all-reduce.12
  629.4 8.3 all-reduce.10
  646.1 9.4 all-reduce.12
  679.4 8.3 all-reduce.10
  687.8 8.3 all-reduce.11
  696.1 9.4 all-reduce.12
  729.5 8.3 all-reduce.10
  737.8 8.3 all-reduce.11
  746.2 9.4 all-reduce.12
  779.5 8.3 all-reduce.10
  796.2 9.4 all-reduce.12
  809.5 162.3 %while.54 = (s32[]{:T(128)}, f32[16,15]{1,0:T(8,128)S(1)}, f32[16]{0:T(128)S(1)}, s32[]{:T(128)}, s32[2]{0:T(128)S(1)}, /*index=5*/s32[1]{0:T(128)}, s32[]{:T(128)}, s32[]{:T(128)}, s32[]{:T(128)}, s32[]{:T(128)}) while((s32[]{:T(128)}, f32[16,15]{1,0:T(8,128)S(1)}, f32[16]{0:T(128)S(1)}, s32[]{:T(128)}, s32[2]{0:T(128)S(1)}, ...), condition=%wide.region_20.21_spmd, body=%wide.region_17.20_spmd.sunk | while | flops 165 | bytes 5167 | solution.py:90
  971.8 59.4 %while.55 = (s32[]{:T(128)}, f32[15]{0:T(128)S(1)}, f32[16]{0:T(128)S(1)}, f32[16,15]{1,0:T(8,128)S(1)}, s32[]{:T(128)}, /*index=5*/s32[]{:T(128)}, s32[]{:T(128)}, s32[]{:T(128)}, s32[]{:T(128)}) while((s32[]{:T(128)}, f32[15]{0:T(128)S(1)}, f32[16]{0:T(128)S(1)}, f32[16,15]{1,0:T(8,128)S(1)}, s32[]{:T(128)}, /*index=5*/s32[]{:T(128)}, ...), condition=%wide.region_23.24_spmd, body=%wide.region_21.23_spmd.sunk | while | flops 43 | bytes 490 | solution.py:97
  (610 shorter events, 483.7 us)
Async XLA Ops:
  1.4 10.8 %collective-permute-start.8 = (f32[2,2,256]{2,1,0:T(2,128)S(1)}, f32[2,2,256]{2,1,0:T(2,128)S(1)}, u32[]{:S(2)}, u32[]{:S(2)}) collective-permute-start(f32[2,2,256]{2,1,0:T(2,128)S(1)} %get-tuple-element.581), channel_id=1, source_target_pairs={{0,64},{64,0},{1,65},{65,1},{2,66},{66,2},{3,67},{67,3},{4,68},{68... | collective-permute-start | bytes 12296 | tf_op jit(solution)/shard_map/ppermute | solution.py:20
  1.4 10.8 %collective-permute-start.9 = (f32[2,2,256]{2,1,0:T(2,128)S(1)}, f32[2,2,256]{2,1,0:T(2,128)S(1)}, u32[]{:S(2)}, u32[]{:S(2)}) collective-permute-start(f32[2,2,256]{2,1,0:T(2,128)S(1)} %get-tuple-element.582), channel_id=1, source_target_pairs={{64,0},{0,64},{65,1},{1,65},{66,2},{2,66},{67,3},{3,67},{68,4},{4,... | collective-permute-start | bytes 12296 | tf_op jit(solution)/shard_map/ppermute | solution.py:22
  3.4 16.6 %collective-permute-start.6 = (f32[68,2]{1,0:T(8,128)S(1)}, f32[68,2]{1,0:T(8,128)S(1)}, u32[]{:S(2)}, u32[]{:S(2)}) collective-permute-start(f32[68,2]{1,0:T(8,128)S(1)} %get-tuple-element.584), channel_id=1, source_target_pairs={{1,0},{2,1},{3,2},{4,3},{5,4},{6,5},{7,6},{8,7},{9,8},{10,9},{11,1... | collective-permute-start | bytes 1640 | tf_op jit(solution)/shard_map/ppermute | solution.py:22
  12.2 9.7 collective-permute-start.7
  12.4 10.3 collective-permute-start.10
  12.4 10.2 collective-permute-start.11
  62.0 1.3 collective-permute-start.1
  63.4 4.0 collective-permute-start.2
  63.4 9.5 collective-permute-start.3
  108.3 1.3 collective-permute-start.1
  109.7 5.5 collective-permute-start.2
  113.5 9.4 collective-permute-start.3
  158.3 1.3 collective-permute-start.1
  159.8 5.5 collective-permute-start.2
  163.6 9.4 collective-permute-start.3
  208.4 1.3 collective-permute-start.1
  209.8 5.5 collective-permute-start.2
  213.6 9.4 collective-permute-start.3
  258.4 1.3 collective-permute-start.1
  259.9 5.5 collective-permute-start.2
  263.7 9.4 collective-permute-start.3
  308.5 1.3 collective-permute-start.1
  309.9 5.5 collective-permute-start.2
  313.7 9.4 collective-permute-start.3
  358.5 1.3 collective-permute-start.1
  360.0 5.5 collective-permute-start.2
  363.8 9.4 collective-permute-start.3
  408.6 1.3 collective-permute-start.1
  410.0 5.5 collective-permute-start.2
  413.8 9.4 collective-permute-start.3
  460.1 5.5 collective-permute-start.2
  463.9 9.4 collective-permute-start.3
  508.7 1.3 collective-permute-start.1
  510.1 5.5 collective-permute-start.2
  513.9 9.4 collective-permute-start.3
  558.8 1.3 collective-permute-start.1
  560.2 5.5 collective-permute-start.2
  564.0 9.4 collective-permute-start.3
  610.2 5.5 collective-permute-start.2
  614.0 9.4 collective-permute-start.3
  658.9 1.3 collective-permute-start.1
  660.3 5.5 collective-permute-start.2
  664.1 9.4 collective-permute-start.3
  708.9 1.3 collective-permute-start.1
  710.3 5.5 collective-permute-start.2
  714.1 9.4 collective-permute-start.3
  760.4 5.5 collective-permute-start.2
  764.2 9.4 collective-permute-start.3
  (26 other events, 46.5 us)
where the time goes:
time: 1040 us
  blocking collectives  475 us (46%)
  waiting for transfers between devices  154 us (15%)
  loops' own time  149 us (14%)
  other arithmetic  84.3 us (8%)
  starting transfers between devices  81.7 us (8%)
  matrix products  46.7 us (4%)
  local copies, waits for them, and re-layouts  42.3 us (4%)
    psum x64, blocking collectives, one_axis_at_a_time(): x = lax.psum(x, axis)  475 us
    ppermute x34, waiting for transfers between devices, padded_2(): lax.ppermute(tail, axis, [(i, (i + 1) % count) for i in range(ends)])  119 us
    another operation x1, loops' own time, least_squares(): lax.fori_loop(0, columns_total, rotate, (hessenberg, target))  97.8 us
    ppermute x34, starting transfers between devices, padded_2(): lax.ppermute(head, axis, [((i + 1) % count, i) for i in range(ends)])  71.7 us
    ppermute x34, waiting for transfers between devices, padded_2(): lax.ppermute(head, axis, [((i + 1) % count, i) for i in range(ends)])  35.2 us
    another operation x46, other arithmetic  30.6 us
    another operation x1, loops' own time, least_squares(): lax.fori_loop(0, columns_total, substitute, jnp.zeros((columns_total,), j...  30.2 us
    dot_general x15, matrix products, arnoldi(): jnp.einsum('kxy,xy->k', basis, applied, precision=lax.Precision.HIGHEST)  26.6 us
  transfers between devices with their start and end apart: 68, of which 64 were waited for; matrix products, arithmetic and copies ran while one was open for 0% of the time, Pallas kernels for 0%

commit v1 on v0

--- a/solution.py
+++ b/solution.py
@@ -28,7 +28,7 @@
 
 def one_axis_at_a_time(x, axes):
     for axis in axes:
-        x = lax.psum(x, axis)
+        x = jnp.sum(lax.all_gather(x, axis), axis=0)
     return x
 
 

time: 1040 us -> 1170 us (1.12)
  local copies, waits for them, and re-layouts: 42.3 us -> 188 us
  waiting for transfers between devices: 154 us -> 94.7 us
  other arithmetic: 84.3 us -> 124 us
  loops' own time: 149 us -> 188 us
  blocking collectives: 475 us -> 452 us
  starting transfers between devices: 81.7 us -> 65.1 us
    psum x64 -> x0, blocking collectives: 475 us -> none  [one_axis_at_a_time(): x = lax.psum(x, axis)]
    while x0 -> x60, blocking collectives: none -> 418 us
    while x30 -> x330, local copies, waits for them, and re-layouts: 0.12 us -> 132 us
    reduce_sum x0 -> x124, other arithmetic: none -> 39.8 us  [one_axis_at_a_time(): x = jnp.sum(lax.all_gather(x, axis), axis=0)]
    another operation x1, loops' own time: 21 us -> 59.5 us  [per_device(): basis, hessenberg = lax.fori_loop(0, RESTART, arnoldi, (basis, hessenberg))]
    ppermute x34, waiting for transfers between devices: 35.2 us -> 0.09 us  [padded_2(): lax.ppermute(head, axis, [((i + 1) % count, i) for i in range(ends)])]
    unnamed x0 -> x4, blocking collectives: none -> 34.2 us
    ppermute x34, waiting for transfers between devices: 119 us -> 94.6 us  [padded_2(): lax.ppermute(tail, axis, [(i, (i + 1) % count) for i in range(ends)])]
  transfers between devices with their start and end apart: 68 -> 68, of which waited for: 64 -> 17; matrix products, arithmetic and copies ran while one was open for 0% -> 3% of each run, Pallas kernels for 0% -> 0%
where the time goes in v1:
time: 1170 us; the launch traced here: 1160 us
  blocking collectives  452 us (39%)
  local copies, waits for them, and re-layouts  188 us (16%)
  loops' own time  188 us (16%)
  other arithmetic  124 us (11%)
  waiting for transfers between devices  94.7 us (8%)
  starting transfers between devices  65.1 us (6%)
  matrix products  46.7 us (4%)
    while x60, blocking collectives  418 us
    while x330, local copies, waits for them, and re-layouts  132 us
    another operation x1, loops' own time, least_squares(): lax.fori_loop(0, columns_total, rotate, (hessenberg, target))  97.9 us
    ppermute x34, waiting for transfers between devices, padded_2(): lax.ppermute(tail, axis, [(i, (i + 1) % count) for i in range(ends)])  94.6 us
    another operation x1, loops' own time, per_device(): basis, hessenberg = lax.fori_loop(0, RESTART, arnoldi, (basis, hessenberg))  59.5 us
    ppermute x34, starting transfers between devices, padded_2(): lax.ppermute(head, axis, [((i + 1) % count, i) for i in range(ends)])  55.1 us
    reduce_sum x124, other arithmetic, one_axis_at_a_time(): x = jnp.sum(lax.all_gather(x, axis), axis=0)  39.8 us
    unnamed x4, blocking collectives  34.2 us
  transfers between devices with their start and end apart: 68, of which 17 were waited for; matrix products, arithmetic and copies ran while one was open for 3% of the time, Pallas kernels for 0%

profile of v1, /device:TPU:0, one launch (start us, length us, event | category | flops | bytes accessed | tf_op | source)
XLA Modules:
  0.0 1159.9 jit_solution(2745572565261197550)
XLA Ops:
  3.9 8.8 collective-permute-start.6
  52.3 16.3 %all-reduce.12 = f32[4]{0:T(128)S(1)} all-reduce(f32[4]{0:T(128)S(1)} %dynamic-update-slice.49), channel_id=1, replica_groups=mesh['gx'=2,'gy_0'=4,'gy_1'=4,'gy_2'=4] {'gy_2'}, use_global_device_ids=true, to_apply=%add.12 | all-reduce | flops 4 | bytes 32
  70.1 863.7 %while.56 = (s32[]{:T(128)}, f32[16,64,256]{2,1,0:T(8,128)S(1)}, f32[16,15]{0,1:T(8,128)S(1)}, f32[64,256]{1,0:T(8,128)S(1)}, f32[64,256]{1,0:T(8,128)S(1)}, /*i...) while((s32[]{:T(128)}, f32[16,64,256]{2,1,0:T(8,128)S(1)}, ...), condition=%wide.region_16.0_spmd.clone, body=%wide.region_5.16_spmd.clone.sunk | while | flops 7373683 | bytes 4416671 | solution.py:135
  91.4 7.7 all-reduce.30
  101.4 7.7 all-reduce.31
  111.3 10.0 all-reduce.32
  149.1 7.7 all-reduce.30
  159.1 7.7 all-reduce.31
  169.1 10.0 all-reduce.32
  206.9 7.7 all-reduce.30
  216.9 7.7 all-reduce.31
  226.8 10.0 all-reduce.32
  264.6 7.7 all-reduce.30
  274.6 7.7 all-reduce.31
  284.6 10.0 all-reduce.32
  322.4 7.7 all-reduce.30
  332.4 7.7 all-reduce.31
  342.3 10.0 all-reduce.32
  380.1 7.7 all-reduce.30
  390.1 7.7 all-reduce.31
  400.1 10.0 all-reduce.32
  437.9 7.7 all-reduce.30
  447.8 7.7 all-reduce.31
  457.8 10.0 all-reduce.32
  495.6 7.7 all-reduce.30
  505.6 7.7 all-reduce.31
  515.6 10.0 all-reduce.32
  553.4 7.7 all-reduce.30
  563.3 7.7 all-reduce.31
  573.3 10.0 all-reduce.32
  611.1 7.7 all-reduce.30
  621.1 7.7 all-reduce.31
  631.1 10.0 all-reduce.32
  668.9 7.7 all-reduce.30
  678.8 7.7 all-reduce.31
  688.8 10.0 all-reduce.32
  726.6 7.7 all-reduce.30
  736.6 7.7 all-reduce.31
  746.6 10.0 all-reduce.32
  784.4 7.7 all-reduce.30
  794.3 7.7 all-reduce.31
  804.3 10.0 all-reduce.32
  842.1 7.7 all-reduce.30
  852.1 7.7 all-reduce.31
  862.1 10.0 all-reduce.32
  919.8 10.0 all-reduce.32
  934.4 162.3 %while.54 = (s32[]{:T(128)}, f32[16,15]{1,0:T(8,128)S(1)}, f32[16]{0:T(128)S(1)}, s32[]{:T(128)}, s32[2]{0:T(128)S(1)}, /*index=5*/s32[1]{0:T(128)}, s32[]{:T(128)}, s32[]{:T(128)}, s32[]{:T(128)}, s32[]{:T(128)}) while((s32[]{:T(128)}, f32[16,15]{1,0:T(8,128)S(1)}, f32[16]{0:T(128)S(1)}, s32[]{:T(128)}, s32[2]{0:T(128)S(1)}, ...), condition=%wide.region_20.21_spmd, body=%wide.region_17.20_spmd.sunk | while | flops 165 | bytes 5167 | solution.py:90
  1096.7 59.4 %while.55 = (s32[]{:T(128)}, f32[15]{0:T(128)S(1)}, f32[16]{0:T(128)S(1)}, f32[16,15]{1,0:T(8,128)S(1)}, s32[]{:T(128)}, /*index=5*/s32[]{:T(128)}, s32[]{:T(128)}, s32[]{:T(128)}, s32[]{:T(128)}) while((s32[]{:T(128)}, f32[15]{0:T(128)S(1)}, f32[16]{0:T(128)S(1)}, f32[16,15]{1,0:T(8,128)S(1)}, s32[]{:T(128)}, /*index=5*/s32[]{:T(128)}, ...), condition=%wide.region_23.24_spmd, body=%wide.region_21.23_spmd.sunk | while | flops 43 | bytes 490 | solution.py:97
  (1114 shorter events, 579.8 us)
Async XLA Ops:
  1.4 11.3 collective-permute-start.8
  1.4 11.3 collective-permute-start.9
  3.9 16.6 %collective-permute-start.6 = (f32[68,2]{1,0:T(8,128)S(1)}, f32[68,2]{1,0:T(8,128)S(1)}, u32[]{:S(2)}, u32[]{:S(2)}) collective-permute-start(f32[68,2]{1,0:T(8,128)S(1)} %get-tuple-element.584), channel_id=1, source_target_pairs={{1,0},{2,1},{3,2},{4,3},{5,4},{6,5},{7,6},{8,7},{9,8},{10,9},{11,1... | collective-permute-start | bytes 1640 | tf_op jit(solution)/shard_map/ppermute | solution.py:22
  12.7 9.4 collective-permute-start.7
  12.9 10.1 collective-permute-start.10
  12.9 10.0 collective-permute-start.11
  70.1 2.5 collective-permute-start
  72.7 5.1 collective-permute-start.2
  72.7 9.5 collective-permute-start.3
  125.3 2.5 collective-permute-start
  127.9 5.7 collective-permute-start.2
  130.5 9.4 collective-permute-start.3
  183.0 2.5 collective-permute-start
  185.7 5.7 collective-permute-start.2
  188.3 9.4 collective-permute-start.3
  240.8 2.5 collective-permute-start
  243.4 5.7 collective-permute-start.2
  246.0 9.4 collective-permute-start.3
  298.5 2.5 collective-permute-start
  301.2 5.7 collective-permute-start.2
  303.8 9.4 collective-permute-start.3
  356.3 2.5 collective-permute-start
  358.9 5.7 collective-permute-start.2
  361.5 9.4 collective-permute-start.3
  414.0 2.5 collective-permute-start
  416.6 5.7 collective-permute-start.2
  419.3 9.4 collective-permute-start.3
  471.8 2.5 collective-permute-start
  474.4 5.7 collective-permute-start.2
  477.0 9.4 collective-permute-start.3
  532.1 5.7 collective-permute-start.2
  534.8 9.4 collective-permute-start.3
  587.3 2.5 collective-permute-start
  589.9 5.7 collective-permute-start.2
  592.5 9.4 collective-permute-start.3
  647.6 5.7 collective-permute-start.2
  650.3 9.4 collective-permute-start.3
  702.8 2.5 collective-permute-start
  705.4 5.7 collective-permute-start.2
  708.0 9.4 collective-permute-start.3
  763.1 5.7 collective-permute-start.2
  765.8 9.4 collective-permute-start.3
  818.3 2.5 collective-permute-start
  820.9 5.7 collective-permute-start.2
  823.5 9.4 collective-permute-start.3
  876.0 2.5 collective-permute-start
  878.6 5.7 collective-permute-start.2
  881.3 9.4 collective-permute-start.3
  (30 other events, 73.8 us)
